TPU v7x, 32 devices: a whole 2x2x4 slice. The times are simulated.
32 devices in a mesh: dp: 4 (over y, x), seq: 8 (over z, core).
Axes of the slice: x: 2, y: 2, z: 4, core: 2. Of those that a mesh axis runs over, the one named last changes fastest.
Arguments:
- tokens: bfloat16 [4, 4096, 2560], P('dp', 'seq'), may hold values from -6 to 6
- w_x: bfloat16 [2560, 3072], P('seq'), may hold values from -0.125 to 0.125
- w_bc: bfloat16 [2560, 256], P('seq'), may hold values from -0.125 to 0.125
- w_dt: bfloat16 [2560, 48], P('seq'), may hold values from -0.125 to 0.125
- dt_bias: float32 [48], replicated, may hold values from -1 to 0.5
- decay_rate: float32 [48], replicated, may hold values from 9.765625e-05 to 0.12
- gain: float32 [3072], replicated, may hold values from 0.5 to 1.5
- cotangent: bfloat16 [4, 4096, 3072], P('dp', 'seq'), may hold values from -0.005859375 to 0.005859375
- counts: int32 [8], replicated, may hold values from 1 to 2, 12 in all
Outputs:
- ssm_output: bfloat16 [4, 4096, 3072], P('dp', 'seq')
- grad_c: float32 [2560, 128], P('seq')
Inputs may be any that keep to these rules, and one draw needn't show every extreme that they name: counts add up to 12 and one of them equals 2.
All inputs are finite; a program needn't handle non-finite values.
Results may differ from a plain program's by a relative error of at most 0.02.
Values may be sent and summed in bfloat16 or wider, within the bound.
A program may use at most 128 MiB of HBM per device.

v0:
```python
import jax
import jax.numpy as jnp
from jax import lax
from jax.sharding import PartitionSpec as P

L = 256


norm_floor = 1.0


def entering(value, axis, join, neutral):
    count, mine = (lax.axis_size(axis), lax.axis_index(axis))
    pieces = jax.tree.map(lambda part: lax.all_gather(part, axis), value)
    subtotal = jax.tree.map(
        lambda part, zero: jnp.full_like(part, 0) + jnp.asarray(zero, part.dtype), value, neutral
    )

    def hop(position, subtotal):
        longer = join(subtotal, jax.tree.map(lambda part: part[position], pieces))
        return jax.tree.map(lambda new, old: jnp.where(position < mine, new, old), longer, subtotal)

    return lax.fori_loop(0, count - 1, hop, subtotal)


def scale_state(state, decay):
    return (state.reshape(decay.shape[0], -1) * decay[:, None]).reshape(state.shape)


def combine_states(earlier, later):
    return (earlier[0] * later[0], scale_state(earlier[1], later[0]) + later[1])


def decay_weights(cumulative, dt_rows):
    length = cumulative.shape[0]
    causal = jnp.arange(length)[:, None] >= jnp.arange(length)[None, :]
    gap_log = cumulative.T[:, :, None] - cumulative.T[:, None, :]
    gap_log = jnp.where(causal[None, :, :], gap_log, -jnp.inf)
    return jnp.exp(gap_log) * dt_rows.T[:, None, :]


def stretch_state(inner, b_proj, dt_rows, a_neg):
    length = inner.shape[0]
    head_count = a_neg.shape[0]
    cumulative = jnp.cumsum(dt_rows * a_neg[None, :], axis=0)
    to_end = jnp.exp(cumulative[-1][None, :] - cumulative) * dt_rows
    scaled = (
        (inner.reshape(length, head_count, -1) * to_end[:, :, None])
        .reshape(length, -1)
        .astype(jnp.bfloat16)
    )
    state_add = jnp.dot(scaled.T, b_proj, preferred_element_type=jnp.float32)
    return (jnp.exp(cumulative[-1]), state_add)


def stretch_outputs(inner, b_proj, c_proj, dt_rows, a_neg, state_in, gain, cot_rows, slot_used):
    length = inner.shape[0]
    head_count = a_neg.shape[0]
    head_size = inner.shape[1] // head_count
    cumulative = jnp.cumsum(dt_rows * a_neg[None, :], axis=0)
    weights = decay_weights(cumulative, dt_rows)
    gram_mat = jnp.dot(c_proj, b_proj.T, preferred_element_type=jnp.float32)
    mixing = (gram_mat[None, :, :] * weights).astype(jnp.bfloat16)
    inner_heads = inner.reshape(length, head_count, head_size)
    y_intra = jnp.einsum("hts,shp->thp", mixing, inner_heads, preferred_element_type=jnp.float32)
    state_low = state_in.astype(jnp.bfloat16)
    growth = jnp.exp(cumulative)[:, :, None]
    y_inter = (
        jnp.dot(c_proj, state_low.T, preferred_element_type=jnp.float32).reshape(
            length, head_count, head_size
        )
        * growth
    )
    full = y_intra + y_inter
    radius = jnp.sqrt(jnp.mean(full * full, axis=2, keepdims=True) + norm_floor)
    gain_heads = gain.reshape(head_count, head_size)
    output = (full / radius * gain_heads * slot_used).reshape(length, -1).astype(jnp.bfloat16)
    grad_out = cot_rows.reshape(length, head_count, head_size) * gain_heads
    grad_full = (
        grad_out / radius
        - full * jnp.sum(grad_out * full, axis=2, keepdims=True) / (head_size * radius**3)
    ) * slot_used
    grad_low = grad_full.astype(jnp.bfloat16)
    intersect = jnp.einsum(
        "thp,shp->hts", grad_low, inner_heads, preferred_element_type=jnp.float32
    )
    combined = jnp.sum(intersect * weights, axis=0).astype(jnp.bfloat16)
    grad_intra = jnp.dot(combined, b_proj, preferred_element_type=jnp.float32)
    scaled_grad = (grad_full * growth).reshape(length, -1).astype(jnp.bfloat16)
    grad_inter = jnp.dot(scaled_grad, state_low, preferred_element_type=jnp.float32)
    return (output, (grad_intra + grad_inter).astype(jnp.bfloat16))


def body(tokens, w_x, w_bc, w_dt, dt_bias, decay_rate, gain, cotangent, counts):
    seq_tokens = tokens[0]
    cot_rows = cotangent[0]
    row_total = seq_tokens.shape[0]
    slot_count = row_total // L
    state_size = w_bc.shape[1] // 2
    head_count = decay_rate.shape[0]
    group_index = lax.axis_index("seq")
    filled = jnp.sum(jnp.where(jnp.arange(counts.shape[0]) == group_index, counts, 0))
    slot_used = (jnp.arange(slot_count) < filled).astype(jnp.float32)
    pieces = (
        lax.all_gather(w_x, "seq", axis=0, tiled=True),
        lax.all_gather(w_bc, "seq", axis=0, tiled=True),
        lax.all_gather(w_dt, "seq", axis=0, tiled=True),
    )
    columns = seq_tokens
    inner_sum, bc_raw, dt_raw = tuple(
        (jnp.dot(columns, block_rows, preferred_element_type=jnp.float32) for block_rows in pieces)
    )
    inner = inner_sum.astype(jnp.bfloat16)
    b_proj = bc_raw[:, :state_size].astype(jnp.bfloat16)
    c_proj = bc_raw[:, state_size:].astype(jnp.bfloat16)
    a_neg = -decay_rate
    dt_blocks = (
        jax.nn.softplus(dt_raw + dt_bias).reshape(slot_count, L, head_count)
        * slot_used[:, None, None]
    )
    inner_blocks = inner.reshape(slot_count, L, -1)
    b_blocks = b_proj.reshape(slot_count, L, -1)
    c_blocks = c_proj.reshape(slot_count, L, -1)
    cot_blocks = cot_rows.reshape(slot_count, L, -1)
    decays, additions = lax.map(
        lambda stretch_data: stretch_state(
            stretch_data[0], stretch_data[1], stretch_data[2], a_neg
        ),
        (inner_blocks, b_blocks, dt_blocks),
    )

    def advance(running, stretch_data):
        return (combine_states(running, stretch_data), running)

    starting_state = (
        jnp.ones((head_count,), jnp.float32),
        jnp.zeros(additions.shape[1:], jnp.float32),
    )
    (dev_decay, dev_state), (prior_decay, prior_state) = lax.scan(
        advance, starting_state, (decays, additions)
    )
    unused_decay, state_before = entering(
        (dev_decay, dev_state), "seq", combine_states, starting_state
    )
    state_in = (state_before.reshape(head_count, -1)[None, :, :] * prior_decay[:, :, None]).reshape(
        prior_state.shape
    ) + prior_state
    outputs, grad_blocks = lax.map(
        lambda stretch_data: stretch_outputs(
            stretch_data[0],
            stretch_data[1],
            stretch_data[2],
            stretch_data[3],
            a_neg,
            stretch_data[4],
            gain,
            stretch_data[5],
            stretch_data[6],
        ),
        (inner_blocks, b_blocks, c_blocks, dt_blocks, state_in, cot_blocks, slot_used),
    )
    ssm_output = outputs.reshape(row_total, -1)
    grad_c_rows = grad_blocks.reshape(row_total, -1)
    columns = seq_tokens
    partial_rows = lax.psum_scatter(
        jnp.dot(columns.T, grad_c_rows, preferred_element_type=jnp.float32).astype(jnp.bfloat16),
        "seq",
        scatter_dimension=0,
        tiled=True,
    )
    gradient = lax.psum(partial_rows, "dp").astype(jnp.float32)
    return (ssm_output[None], gradient)


def solution(mesh):
    return jax.shard_map(
        body,
        mesh=mesh,
        in_specs=(
            P("dp", "seq", None),
            P("seq", None),
            P("seq", None),
            P("seq", None),
            P(),
            P(),
            P(),
            P("dp", "seq", None),
            P(),
        ),
        out_specs=(P("dp", "seq", None), P("seq", None)),
        check_vma=False,
    )
```

profile of v0, /device:TPU:9, one launch (start us, length us, event | category | flops | bytes accessed | tf_op | source)
XLA Modules:
  0.0 517.9 jit_solution(12384996486794329397)
XLA Ops:
  7.3 0.7 all-gather.9.cloned.1.call-update
  8.0 0.7 all-gather.7.cloned.1.call-update
  8.8 16.0 %all-gather.2 = bf16[8,320,48]{1,2,0:T(8,128)(2,1)S(1)} all-gather(bf16[1,320,48]{1,2,0:T(8,128)(2,1)} %bitcast.250), channel_id=1, replica_groups=mesh['dp'=4,'seq'=8] {'seq'}, dimensions={0}, use_global_device_ids=true | all-gather | bytes 276480 | tf_op jit(solution)/shard_map/all_gather | solution.py:107
  25.1 0.6 fusion.65
  25.7 0.6 compare_convert_fusion
  26.4 0.9 compare_select_fusion
  27.4 6.9 %all-gather.9.cloned.1.call-done = bf16[2560,256]{1,0:T(8,128)(2,1)} async-done(((bf16[320,256]{1,0:T(8,128)(2,1)}), bf16[2560,256]{1,0:T(8,128)(2,1)}) %all-gather.9.cloned.1.call-update) | async-done | bytes 1310736 | tf_op jit(solution)/shard_map/all_gather | solution.py:106
  34.3 2.2 fusion.57
  36.5 139.4 %all-gather.7.cloned.1.call-done = bf16[2560,3072]{1,0:T(8,128)(2,1)} async-done(((bf16[320,3072]{1,0:T(8,128)(2,1)}), bf16[2560,3072]{1,0:T(8,128)(2,1)}) %all-gather.7.cloned.1.call-update) | async-done | bytes 15728656 | tf_op jit(solution)/shard_map/all_gather | solution.py:105
  175.9 12.8 %convolution_convert_fusion = bf16[512,3072]{1,0:T(8,128)(2,1)} fusion(bf16[2560,3072]{1,0:T(8,128)(2,1)} %all-gather.7.cloned.1.call-done, bf16[1,512,2560]{2,1,0:T(8,128)(2,1)S(1)} %copy-done), kind=kOutput, calls=%fused_computation.87 | convolution fusion | flops 8054636544 | bytes 21495808 | tf_op jit(solution)/shard_map/dot_general | solution.py:111
  188.8 4.7 copy.52
  193.5 1.9 broadcast.81.clone
  195.3 11.9 %while.55 = (s32[]{:T(128)}, f32[2,48]{1,0:T(2,128)S(1)}, f32[2,3072,128]{2,1,0:T(8,128)}, f32[2,256,48]{1,2,0:T(8,128)S(1)}, f32[48]{0:T(128)S(1)}, /*index=5*/...) while((s32[]{:T(128)}, f32[2,48]{1,0:T(2,128)S(1)}, ...), condition=%wide.region_4.5_spmd, body=%wide.region_1.4_spmd.sunk | while | flops 205308048 | bytes 35166580 | solution.py:125
  195.4 0.6 reduce-window.28
  196.6 1.7 constant_dynamic-slice_fusion.7
  199.5 1.7 copy-done.6
  201.4 0.6 reduce-window.28
  202.6 1.7 constant_dynamic-slice_fusion.7
  205.5 1.7 copy-done.6
  207.3 1.9 broadcast.81
  209.2 10.4 %while.57 = (s32[]{:T(128)}, f32[48]{0:T(128)S(1)}, f32[3072,128]{1,0:T(8,128)}, f32[2,48]{1,0:T(2,128)S(1)}, f32[2,3072,128]{2,1,0:T(8,128)}, /*index=5*/f32[2,...) while((s32[]{:T(128)}, f32[48]{0:T(128)S(1)}, f32[3072,128]{1,0:T(8,128)}, ...), condition=%wide.region_6.7_spmd.clone, body=%wide.region_5.6_spmd.clone.sunk | while | flops 1572963 | bytes 20498576 | solution.py:139
  209.3 1.3 bitcast_dynamic-update-slice_fusion.2
  210.6 1.2 copy-done.7
  211.8 1.6 bitcast_add_fusion.4
  213.6 2.9 bitcast_dynamic-update-slice_fusion.2
  216.5 3.0 bitcast_add_fusion.4
  221.1 13.0 %all-reduce = f32[384]{0:T(512)S(1)} all-reduce(f32[384]{0:T(512)S(1)} %dynamic-update-slice), channel_id=2, replica_groups=mesh['dp'=4,'seq'=8] {'seq'}, use_global_device_ids=true, to_apply=%add | all-reduce | flops 384 | bytes 3072
  234.3 100.4 %all-gather.11.cloned.1.call-done = f32[24576,128]{1,0:T(8,128)} async-done(((f32[3072,128]{1,0:T(8,128)}), f32[24576,128]{1,0:T(8,128)}) %all-gather.11.cloned.1.call-update) | async-done | bytes 12582928 | tf_op jit(solution)/shard_map/all_gather | solution.py:14
  334.7 25.4 %while.58 = (s32[]{:T(128)}, f32[3072,128]{1,0:T(8,128)}, s32[]{:T(128)}, f32[8,48]{1,0:T(8,128)S(1)}, f32[8,3072,128]{2,1,0:T(8,128)}, /*index=5*/s32[]{:T(128)}, s32[]{:T(128)}) while((s32[]{:T(128)}, f32[3072,128]{1,0:T(8,128)}, s32[]{:T(128)}, f32[8,48]{1,0:T(8,128)S(1)}, f32[8,3072,128]{2,1,0:T(8,128)}, /*index=5*/s32[]{:T(128)}, ...), condition=%wide.region_8.9_spmd.clone, body=%wide.region_7.8_spmd.clone.sunk | while | flops 1572868 | bytes 4768425 | solution.py:23
  334.9 3.1 fusion.128
  338.1 3.5 fusion.128
  341.8 3.5 fusion.128
  345.5 3.5 fusion.128
  349.2 3.5 fusion.128
  352.9 3.5 fusion.128
  356.6 3.5 fusion.128
  360.1 3.7 multiply_add_fusion
  363.8 68.5 %while.56 = (s32[]{:T(128)}, bf16[2,256,3072]{2,1,0:T(8,128)(2,1)}, bf16[2,256,128]{2,1,0:T(8,128)(2,1)S(1)}, bf16[2,256,3072]{1,2,0:T(8,128)(2,1)}, bf16[2,256,...) while((s32[]{:T(128)}, bf16[2,256,3072]{2,1,0:T(8,128)(2,1)}, ...), condition=%wide.region_15.16_spmd, body=%wide.region_9.15_spmd.sunk | while | flops 1291211008 | bytes 81402336 | solution.py:148
  363.9 0.6 reduce-window.30
  364.8 1.3 dynamic-slice_convert_fusion.3
  367.2 5.8 %multiply_reduce_fusion.4 = (f32[256,48]{0,1:T(8,128)S(1)}, f32[256,48,64]{0,2,1:T(8,128)}) fusion(f32[256,48,64]{0,2,1:T(8,128)S(1)} %fusion.122, f32[256,48]{0,1:T(8,128)S(1)} %exponential_bitcast_fusion.2, bf16[256,48,64]{0,2,1:T(8,128)(2,1)S(1)} %bitcast.241, f32[48,256]{1,0:T(8,128)S(1)} %dynamic-slice_bitcast_fusion.4, ...), kind=kOutput, calls=%fused_computation.46.clone.1 | convolution fusion | flops 421515264 | bytes 8388608 | tf_op jit(solution)/shard_map/while/body/eval_jaxpr/hts,shp->thp/dot_general | solution.py:65
  373.0 0.6 dynamic_slice.132
  373.7 3.7 multiply_convert_fusion.8
  377.4 2.7 copy.93
  380.1 3.7 constant_dynamic-slice_fusion.9
  383.8 2.6 copy.94
  386.4 6.2 %multiply_convert_fusion.9 = (bf16[256,48,64]{0,2,1:T(8,128)(2,1)S(1)}, bf16[256,48,64]{0,2,1:T(8,128)(2,1)S(1)}) fusion(f32[256,48]{0,1:T(8,128)S(1)} %exponential_bitcast_fusion.2, f32[]{:T(128)} %bitcast.227, f32[256,48]{0,1:T(8,128)S(1)} %get-tuple-element.669, f32[256,48,64]{0,2,1:T(8,128)} %get-tuple-element.665, ...), kind=kOutput, calls=%fused_computation.44.clone.1 | output fusion | flops 10235967 | bytes 8024068 | tf_op jit(solution)/shard_map/while/body/eval_jaxpr/mul | solution.py:81
  392.6 4.6 multiply_reduce_fusion.5
  397.4 0.6 fusion.126
  399.1 1.3 dynamic-slice_convert_fusion.3
  401.4 5.8 %multiply_reduce_fusion.4 = (f32[256,48]{0,1:T(8,128)S(1)}, f32[256,48,64]{0,2,1:T(8,128)}) fusion(f32[256,48,64]{0,2,1:T(8,128)S(1)} %fusion.122, f32[256,48]{0,1:T(8,128)S(1)} %exponential_bitcast_fusion.2, bf16[256,48,64]{0,2,1:T(8,128)(2,1)S(1)} %bitcast.241, f32[48,256]{1,0:T(8,128)S(1)} %dynamic-slice_bitcast_fusion.4, ...), kind=kOutput, calls=%fused_computation.46.clone.1 | convolution fusion | flops 421515264 | bytes 8388608 | tf_op jit(solution)/shard_map/while/body/eval_jaxpr/hts,shp->thp/dot_general | solution.py:65
  407.3 0.6 dynamic_slice.132
  408.0 3.7 multiply_convert_fusion.8
  411.7 2.7 copy.93
  414.4 3.7 constant_dynamic-slice_fusion.9
  418.1 2.6 copy.94
  420.7 6.2 %multiply_convert_fusion.9 = (bf16[256,48,64]{0,2,1:T(8,128)(2,1)S(1)}, bf16[256,48,64]{0,2,1:T(8,128)(2,1)S(1)}) fusion(f32[256,48]{0,1:T(8,128)S(1)} %exponential_bitcast_fusion.2, f32[]{:T(128)} %bitcast.227, f32[256,48]{0,1:T(8,128)S(1)} %get-tuple-element.669, f32[256,48,64]{0,2,1:T(8,128)} %get-tuple-element.665, ...), kind=kOutput, calls=%fused_computation.44.clone.1 | output fusion | flops 10235967 | bytes 8024068 | tf_op jit(solution)/shard_map/while/body/eval_jaxpr/mul | solution.py:81
  426.9 4.6 multiply_reduce_fusion.5
  431.7 0.6 fusion.126
  432.9 1.1 copy.56
  434.0 26.0 %reduce-scatter.4.cloned.1.call-done = bf16[320,128]{1,0:T(8,128)(2,1)} async-done(((bf16[2560,128]{1,0:T(8,128)(2,1)}), bf16[320,128]{1,0:T(8,128)(2,1)}) %reduce-scatter.4.cloned.1.call-update) | async-done | bytes 81936
  460.0 1.6 copy.57
  461.7 48.0 %all-reduce.3.cloned.1.call-done = bf16[320,128]{0,1:T(8,128)(2,1)} async-done(((bf16[320,128]{0,1:T(8,128)(2,1)}), bf16[320,128]{0,1:T(8,128)(2,1)}) %all-reduce.3.cloned.1.call-update) | async-done | bytes 81936 | tf_op jit(solution)/shard_map/psum | solution.py:171
  509.7 1.7 copy.55
  (144 shorter events, 11.6 us)
Async XLA Ops:
  7.2 19.2 %copy-start = (bf16[1,512,2560]{2,1,0:T(8,128)(2,1)S(1)}, bf16[1,512,2560]{2,1,0:T(8,128)(2,1)}, u32[]{:S(2)}) copy-start(bf16[1,512,2560]{2,1,0:T(8,128)(2,1)} %param.17) | copy-start | bytes 7864324
  7.2 17.9 %copy-start.10 = (f32[48]{0:T(128)S(1)}, f32[48]{0:T(128)}, u32[]{:S(2)}) copy-start(f32[48]{0:T(128)} %param.22) | copy-start | bytes 580
  7.2 17.9 %copy-start.11 = (s32[8]{0:T(128)S(1)}, s32[8]{0:T(128)}, u32[]{:S(2)}) copy-start(s32[8]{0:T(128)} %param.25) | copy-start | bytes 100
  7.2 19.2 %copy-start.9 = (f32[48]{0:T(128)S(1)}, f32[48]{0:T(128)}, u32[]{:S(2)}) copy-start(f32[48]{0:T(128)} %param.21) | copy-start | bytes 580
  7.2 27.1 %all-gather.9.cloned.1.call-start = ((), (), s32[]{:S(2)}) async-start(), calls=%async_computation.2 | async-start | bytes 1474560 | tf_op jit(solution)/shard_map/all_gather | solution.py:106
  7.9 168.0 %all-gather.7.cloned.1.call-start = ((), (), s32[]{:S(2)}) async-start(), calls=%async_computation.1 | async-start | bytes 17694720 | tf_op jit(solution)/shard_map/all_gather | solution.py:105
  8.7 326.1 %all-gather.11.cloned.1.call-start = ((), (), s32[]{:S(2)}) async-start(), calls=%async_computation.4 | async-start | bytes 14155776 | tf_op jit(solution)/shard_map/all_gather | solution.py:14
  196.6 2.4 copy-start.5
  199.5 1.7 copy-start.6
  202.6 2.4 copy-start.5
  205.5 1.7 copy-start.6
  209.2 10.5 %copy-start.12 = (u32[32]{0:T(128)S(1)}, u32[32]{0:T(128)}, u32[]{:S(2)}) copy-start(u32[32]{0:T(128)} %constant.99) | copy-start | bytes 388
  209.3 2.5 copy-start.7
  213.6 2.9 copy-start.7
  219.6 240.4 %reduce-scatter.4.cloned.1.call-start = ((), (), s32[]{:S(2)}) async-start(), calls=%async_computation.5 | async-start | bytes 737280
  360.1 3.7 copy-start.8
  364.7 2.3 copy-start.1
  367.1 5.9 %copy-start.3 = (bf16[1,256,3072]{1,2,0:T(8,128)(2,1)}, bf16[1,256,3072]{1,2,0:T(8,128)(2,1)S(1)}, u32[]{:S(2)}) copy-start(bf16[1,256,3072]{1,2,0:T(8,128)(2,1)S(1)} %constant_dynamic-slice_fusion.8) | copy-start | bytes 4718596 | tf_op jit(solution)/shard_map/while
  386.4 6.2 %copy-start.4 = (bf16[1,256,3072]{1,2,0:T(8,128)(2,1)S(1)}, bf16[1,256,3072]{1,2,0:T(8,128)(2,1)}, u32[]{:S(2)}) copy-start(bf16[1,256,3072]{1,2,0:T(8,128)(2,1)} %copy-done.3) | copy-start | bytes 4718596 | tf_op jit(solution)/shard_map/while
  392.6 4.8 copy-start.2
  398.9 2.3 copy-start.1
  401.4 5.9 %copy-start.3 = (bf16[1,256,3072]{1,2,0:T(8,128)(2,1)}, bf16[1,256,3072]{1,2,0:T(8,128)(2,1)S(1)}, u32[]{:S(2)}) copy-start(bf16[1,256,3072]{1,2,0:T(8,128)(2,1)S(1)} %constant_dynamic-slice_fusion.8) | copy-start | bytes 4718596 | tf_op jit(solution)/shard_map/while
  420.7 6.2 %copy-start.4 = (bf16[1,256,3072]{1,2,0:T(8,128)(2,1)S(1)}, bf16[1,256,3072]{1,2,0:T(8,128)(2,1)}, u32[]{:S(2)}) copy-start(bf16[1,256,3072]{1,2,0:T(8,128)(2,1)} %copy-done.3) | copy-start | bytes 4718596 | tf_op jit(solution)/shard_map/while
  426.9 4.8 copy-start.2
  434.0 75.7 %all-reduce.3.cloned.1.call-start = ((), (), s32[]{:S(2)}) async-start(), calls=%async_computation.3 | async-start | bytes 196608 | tf_op jit(solution)/shard_map/psum | solution.py:171
Sparse Core Ops, SparseCore 0:
  9.7 24.6 all-gather.8
  36.0 139.9 all-gather.6
  219.7 115.0 all-gather.10
  434.1 25.8 reduce-scatter.3
  463.3 46.3 all-reduce.2
where the time goes:
time: 521 us; the launch traced here: 518 us
  waiting for transfers between devices  322 us (62%)
  other arithmetic  62.6 us (12%)
  local copies, waits for them, and re-layouts  47.4 us (9%)
  matrix products  41.5 us (8%)
  blocking collectives  29 us (6%)
  between operations  14.6 us (3%)
    all_gather x1, waiting for transfers between devices, body(): lax.all_gather(w_x, 'seq', axis=0, tiled=True)  139 us
    all_gather x1, waiting for transfers between devices, entering(): pieces = jax.tree.map(lambda part: lax.all_gather(part, axis), value)  100 us
    psum x1, waiting for transfers between devices, body(): gradient = lax.psum(partial_rows, 'dp').astype(jnp.float32)  48 us
    unnamed x6, waiting for transfers between devices  27.4 us
    select_n x7, other arithmetic, hop(): jnp.where(position < mine, new, old)  24.3 us
    dynamic_slice x8, local copies, waits for them, and re-layouts, body(): lax.map(lambda stretch_data: stretch_state(stretch_data[0], stretch_data[...  16.2 us
    all_gather x1, blocking collectives, body(): lax.all_gather(w_dt, 'seq', axis=0, tiled=True)  16 us
    dot_general x3, matrix products, body(): jnp.dot(columns, block_rows, preferred_element_type=jnp.float32)  15.9 us
  transfers between devices with their start and end apart: 5, of which 5 were waited for; matrix products, arithmetic and copies ran while one was open for 1% of the time, Pallas kernels for 0%

commit v1 on v0

v1 whole, which is shorter than its diff:
```python
import functools

import jax
import jax.numpy as jnp
from jax import lax
from jax.experimental import pallas as pl
from jax.experimental.pallas import tpu as pltpu
from jax.sharding import PartitionSpec as P

L = 256
LANES = 128
MESH = pl.DeviceIdType.MESH
VMEM_LIMIT = 60 * 1024 * 1024

norm_floor = 1.0


def greet(partners):
    barrier = pltpu.get_barrier_semaphore()
    for partner in partners:
        pl.semaphore_signal(barrier, inc=1, device_id=partner, device_id_type=MESH)
    pl.semaphore_wait(barrier, len(partners))


def wait_bytes(view, sem):
    pltpu.make_async_copy(view, view, sem).wait()


def project_kernel(
    seq_size, stages, tok_ref, wm_ref, we_ref, inner_ref, ext_ref,
    buf_e, buf_m, local_sem, send_sem, ring_sem, side_sem, pair_sem,
):
    dp, seq = lax.axis_index("dp"), lax.axis_index("seq")
    chips = seq_size // 2
    reach = chips // 2
    chip, core = seq // 2, seq % 2
    part = wm_ref.shape[0]
    half = (dp + dp // 2) % 2
    right = (dp, lax.rem(chip + 1, chips) * 2 + core)
    left = (dp, lax.rem(chip + chips - 1, chips) * 2 + core)
    side = (
        (dp + 1 - 2 * (dp % 2), seq),
        (dp + 2 - 4 * ((dp // 2) % 2), seq),
    )
    sibling = (dp, seq + 1 - 2 * core)

    def rows(offset):
        owner = lax.rem(chip + offset + chips, chips) * 2 + core
        return pl.ds(pl.multiple_of(owner * part, 16), part)

    def chunk(stage, slot, offset):
        if stage == 0:
            return buf_e.at[slot, rows(offset), :]
        return buf_m.at[slot * (stages - 1) + stage - 1, rows(offset), :]

    def sample(stage, slots, count):
        buf = buf_e if stage == 0 else buf_m
        return buf.at[pl.ds(0, slots), pl.ds(0, count * part), :]

    def send(stage, slot, offset, target, sem):
        view = chunk(stage, slot, offset)
        pltpu.make_async_remote_copy(
            src_ref=view, dst_ref=view, send_sem=send_sem.at[min(stage, 1)], recv_sem=sem,
            device_id=target, device_id_type=MESH,
        ).start()

    wide = buf_m.shape[2]
    slim = buf_e.shape[2]
    for stage in range(stages):
        for slot in range(4):
            if stage == 0:
                source = we_ref.at[:, pl.ds(slot * slim, slim)]
            else:
                source = wm_ref.at[:, pl.ds((slot * (stages - 1) + stage - 1) * wide, wide)]
            pltpu.make_async_copy(source, chunk(stage, slot, 0), local_sem.at[stage]).start()
    greet((right, left, sibling) + side)

    def quarters(direction, distance):
        return (0, 1) if distance < reach else (direction,)

    def own(stage):
        wait_bytes(sample(stage, 4, 1), local_sem.at[stage])
        for direction, target in ((0, right), (1, left)):
            for quarter in quarters(direction, 1):
                send(stage, half * 2 + quarter, 0, target, ring_sem.at[direction, stage, 0])
        for slot in range(4):
            send(stage, slot, 0, sibling, pair_sem.at[stage])

    def ring(stage, distance):
        for direction, target in ((0, right), (1, left)):
            got = quarters(direction, distance)
            offset = -distance if direction == 0 else distance
            wait_bytes(sample(stage, len(got), 1), ring_sem.at[direction, stage, distance - 1])
            if distance < reach:
                for quarter in quarters(direction, distance + 1):
                    send(
                        stage, half * 2 + quarter, offset, target,
                        ring_sem.at[direction, stage, distance],
                    )
            for quarter in got:
                send(stage, half * 2 + quarter, offset, side[quarter], side_sem.at[stage])
            for quarter in got:
                send(stage, half * 2 + quarter, offset, sibling, pair_sem.at[stage])

    def cross(stage):
        wait_bytes(sample(stage, 2, chips - 1), side_sem.at[stage])
        for offset in range(1, chips):
            for quarter in range(2):
                send(stage, (1 - half) * 2 + quarter, offset, sibling, pair_sem.at[stage])

    def multiply(stage):
        wait_bytes(sample(stage, 4, chips), pair_sem.at[stage])

        @pl.loop(0, 4)
        def _(slot):
            if stage == 0:
                ext_ref[:, pl.ds(pl.multiple_of(slot * slim, slim), slim)] = jnp.dot(
                    tok_ref[...], buf_e[slot], preferred_element_type=jnp.float32
                )
            else:
                index = slot * (stages - 1) + stage - 1
                inner_ref[:, pl.ds(pl.multiple_of(index * wide, wide), wide)] = jnp.dot(
                    tok_ref[...], buf_m[index], preferred_element_type=jnp.float32
                ).astype(jnp.bfloat16)

    tasks = []
    for stage in range(stages):
        for distance in range(1, reach + 1):
            tasks.append((stage * reach + distance, "ring", stage, distance))
        tasks.append((stage * reach + reach + 1.5, "cross", stage, 0))
        tasks.append((stage * reach + reach + 3.2, "multiply", stage, 0))
    own(0)
    own(1)
    for _, kind, stage, distance in sorted(tasks):
        if kind == "ring":
            ring(stage, distance)
            if distance == 1 and stage + 2 < stages:
                own(stage + 2)
        elif kind == "cross":
            cross(stage)
        else:
            multiply(stage)
    wait_bytes(sample(0, 4, seq_size - 1), send_sem.at[0])
    wait_bytes(sample(1, 4 * (stages - 1), seq_size - 1), send_sem.at[1])


def project(seq_tokens, w_main, w_ext, seq_size):
    total, depth = seq_tokens.shape
    width = w_main.shape[1]
    stages = 4
    wide = width // (4 * (stages - 1))
    slim = w_ext.shape[1] // 4
    reach = seq_size // 4
    vmem = pl.BlockSpec(memory_space=pltpu.VMEM)
    hbm = pl.BlockSpec(memory_space=pl.ANY)
    return pl.pallas_call(
        functools.partial(project_kernel, seq_size, stages),
        out_shape=(
            jax.ShapeDtypeStruct((total, width), jnp.bfloat16),
            jax.ShapeDtypeStruct((total, 4 * slim), jnp.float32),
        ),
        in_specs=[vmem, hbm, hbm],
        out_specs=(vmem, vmem),
        scratch_shapes=[
            pltpu.VMEM((4, depth, slim), jnp.bfloat16),
            pltpu.VMEM((4 * (stages - 1), depth, wide), jnp.bfloat16),
            pltpu.SemaphoreType.DMA((stages,)),
            pltpu.SemaphoreType.DMA((2,)),
            pltpu.SemaphoreType.DMA((2, stages, reach)),
            pltpu.SemaphoreType.DMA((stages,)),
            pltpu.SemaphoreType.DMA((stages,)),
        ],
        compiler_params=pltpu.CompilerParams(
            collective_id=0, has_side_effects=True, vmem_limit_bytes=VMEM_LIMIT
        ),
        name="project",
    )(seq_tokens, w_main, w_ext)


def others(axis_size, me):
    return [lax.rem(me + step, axis_size) for step in range(1, axis_size)]


def entering_kernel(
    seq_size, add_ref, decay_ref, enter_ref, adds, decays, back, local_sem, send_sem, recv_sem
):
    dp, seq = lax.axis_index("dp"), lax.axis_index("seq")
    width = adds.shape[2]

    def columns(index):
        return pl.ds(pl.multiple_of(index * width, LANES), width)

    peers = others(seq_size, seq)
    own = (
        pltpu.make_async_copy(add_ref.at[:, columns(seq)], adds.at[seq], local_sem.at[0]),
        pltpu.make_async_copy(decay_ref.at[:, columns(seq)], decays.at[seq], local_sem.at[1]),
    )
    for copy in own:
        copy.start()
    greet([(dp, peer) for peer in peers])
    copies = []
    for step, peer in enumerate(peers):
        for kind, (source, target) in enumerate(((decay_ref, decays), (add_ref, adds))):
            copy = pltpu.make_async_remote_copy(
                src_ref=source.at[:, columns(peer)], dst_ref=target.at[seq],
                send_sem=send_sem.at[kind, step], recv_sem=recv_sem.at[kind, step],
                device_id=(dp, peer), device_id_type=MESH,
            )
            copy.start()
            copies.append(copy)
    for copy in copies:
        copy.wait()
    for copy in own:
        copy.wait()
    running = jnp.zeros(adds.shape[1:], jnp.float32)
    for index in range(seq_size):
        back[index] = running.astype(jnp.bfloat16)
        if index + 1 < seq_size:
            running = running * decays[index][0:1, :] + adds[index].astype(jnp.float32)
    mine = pltpu.make_async_copy(back.at[seq], enter_ref.at[:, columns(seq)], local_sem.at[2])
    mine.start()
    copies = []
    for step, peer in enumerate(peers):
        copy = pltpu.make_async_remote_copy(
            src_ref=back.at[peer], dst_ref=enter_ref.at[:, columns(seq)],
            send_sem=send_sem.at[2, step], recv_sem=recv_sem.at[2, step],
            device_id=(dp, peer), device_id_type=MESH,
        )
        copy.start()
        copies.append(copy)
    for copy in copies:
        copy.wait()
    mine.wait()


def entering(addition, decay, seq_size):
    state_size, width = addition.shape
    blocks = -(-width // LANES)
    each = -(-blocks // seq_size) * LANES
    padding = each * seq_size - width
    if padding:
        addition = jnp.pad(addition, ((0, 0), (0, padding)))
        decay = jnp.pad(decay, ((0, 0), (0, padding)))
    hbm = pl.BlockSpec(memory_space=pl.ANY)
    vmem = pl.BlockSpec(memory_space=pltpu.VMEM)
    result = pl.pallas_call(
        functools.partial(entering_kernel, seq_size),
        out_shape=jax.ShapeDtypeStruct((state_size, each * seq_size), jnp.bfloat16),
        in_specs=[hbm, hbm],
        out_specs=hbm,
        scratch_shapes=[
            pltpu.VMEM((seq_size, state_size, each), jnp.bfloat16),
            pltpu.VMEM((seq_size, decay.shape[0], each), jnp.float32),
            pltpu.VMEM((seq_size, state_size, each), jnp.bfloat16),
            pltpu.SemaphoreType.DMA((3,)),
            pltpu.SemaphoreType.DMA((3, seq_size)),
            pltpu.SemaphoreType.DMA((3, seq_size)),
        ],
        compiler_params=pltpu.CompilerParams(
            collective_id=1, has_side_effects=True, vmem_limit_bytes=VMEM_LIMIT
        ),
        name="entering",
    )(addition, decay)
    return result[:, :width]


def reduce_kernel(
    seq_size, dp_size, part_ref, out_ref, landed, total, across, local_sem, send_sem, recv_sem,
    dp_send_sem, dp_recv_sem,
):
    dp, seq = lax.axis_index("dp"), lax.axis_index("seq")
    height = out_ref.shape[0]

    def rows(index):
        return pl.ds(pl.multiple_of(index * height, 16), height)

    peers = others(seq_size, seq)
    fellows = others(dp_size, dp)
    own = pltpu.make_async_copy(part_ref.at[rows(seq), :], landed.at[0], local_sem)
    own.start()
    greet([(dp, peer) for peer in peers] + [(fellow, seq) for fellow in fellows])
    copies = []
    for step, peer in enumerate(peers):
        copy = pltpu.make_async_remote_copy(
            src_ref=part_ref.at[rows(peer), :], dst_ref=landed.at[step + 1],
            send_sem=send_sem.at[step], recv_sem=recv_sem.at[step],
            device_id=(dp, peer), device_id_type=MESH,
        )
        copy.start()
        copies.append(copy)
    own.wait()
    for copy in copies:
        copy.wait()
    mine = landed[0].astype(jnp.float32)
    for step in range(1, seq_size):
        mine = mine + landed[step].astype(jnp.float32)
    total[...] = mine.astype(jnp.bfloat16)
    copies = []
    for step, fellow in enumerate(fellows):
        copy = pltpu.make_async_remote_copy(
            src_ref=total, dst_ref=across.at[step],
            send_sem=dp_send_sem.at[step], recv_sem=dp_recv_sem.at[step],
            device_id=(fellow, seq), device_id_type=MESH,
        )
        copy.start()
        copies.append(copy)
    for copy in copies:
        copy.wait()
    mine = total[...].astype(jnp.float32)
    for step in range(dp_size - 1):
        mine = mine + across[step].astype(jnp.float32)
    out_ref[...] = mine


def reduce_rows(partial, seq_size, dp_size):
    height = partial.shape[0] // seq_size
    width = partial.shape[1]
    hbm = pl.BlockSpec(memory_space=pl.ANY)
    vmem = pl.BlockSpec(memory_space=pltpu.VMEM)
    return pl.pallas_call(
        functools.partial(reduce_kernel, seq_size, dp_size),
        out_shape=jax.ShapeDtypeStruct((height, width), jnp.float32),
        in_specs=[hbm],
        out_specs=vmem,
        scratch_shapes=[
            pltpu.VMEM((seq_size, height, width), jnp.bfloat16),
            pltpu.VMEM((height, width), jnp.bfloat16),
            pltpu.VMEM((dp_size - 1, height, width), jnp.bfloat16),
            pltpu.SemaphoreType.DMA,
            pltpu.SemaphoreType.DMA((seq_size - 1,)),
            pltpu.SemaphoreType.DMA((seq_size - 1,)),
            pltpu.SemaphoreType.DMA((dp_size - 1,)),
            pltpu.SemaphoreType.DMA((dp_size - 1,)),
        ],
        compiler_params=pltpu.CompilerParams(
            collective_id=2, has_side_effects=True, vmem_limit_bytes=VMEM_LIMIT
        ),
        name="reduce_rows",
    )(partial)


def decay_weights(cumulative, dt_rows):
    length = cumulative.shape[0]
    causal = jnp.arange(length)[:, None] >= jnp.arange(length)[None, :]
    gap_log = cumulative.T[:, :, None] - cumulative.T[:, None, :]
    gap_log = jnp.where(causal[None, :, :], gap_log, -jnp.inf)
    return jnp.exp(gap_log) * dt_rows.T[:, None, :]


def stretch_state(inner, b_proj, cumulative, dt_rows, head_size):
    to_end = jnp.exp(cumulative[-1][None, :] - cumulative) * dt_rows
    scaled = (inner * jnp.repeat(to_end, head_size, axis=1)).astype(jnp.bfloat16)
    return jnp.dot(b_proj.T, scaled, preferred_element_type=jnp.float32)


def stretch_outputs(inner, b_proj, c_proj, cumulative, dt_rows, state_low, gain, cot_rows, used):
    length = inner.shape[0]
    head_count = cumulative.shape[1]
    head_size = inner.shape[1] // head_count
    weights = decay_weights(cumulative, dt_rows)
    gram_mat = jnp.dot(c_proj, b_proj.T, preferred_element_type=jnp.float32)
    mixing = (gram_mat[None, :, :] * weights).astype(jnp.bfloat16)
    inner_heads = inner.reshape(length, head_count, head_size)
    y_intra = jnp.einsum("hts,shp->thp", mixing, inner_heads, preferred_element_type=jnp.float32)
    growth = jnp.exp(cumulative)[:, :, None]
    y_inter = (
        jnp.dot(c_proj, state_low, preferred_element_type=jnp.float32).reshape(
            length, head_count, head_size
        )
        * growth
    )
    full = y_intra + y_inter
    radius = jnp.sqrt(jnp.mean(full * full, axis=2, keepdims=True) + norm_floor)
    gain_heads = gain.reshape(head_count, head_size)
    output = (full / radius * gain_heads * used).reshape(length, -1).astype(jnp.bfloat16)
    grad_out = cot_rows.reshape(length, head_count, head_size) * gain_heads
    grad_full = (
        grad_out / radius
        - full * jnp.sum(grad_out * full, axis=2, keepdims=True) / (head_size * radius**3)
    ) * used
    grad_low = grad_full.astype(jnp.bfloat16)
    intersect = jnp.einsum(
        "thp,shp->hts", grad_low, inner_heads, preferred_element_type=jnp.float32
    )
    combined = jnp.sum(intersect * weights, axis=0).astype(jnp.bfloat16)
    grad_intra = jnp.dot(combined, b_proj, preferred_element_type=jnp.float32)
    scaled_grad = (grad_full * growth).reshape(length, -1).astype(jnp.bfloat16)
    grad_inter = jnp.dot(scaled_grad, state_low.T, preferred_element_type=jnp.float32)
    return (output, (grad_intra + grad_inter).astype(jnp.bfloat16))


def body(dp_size, seq_size, tokens, w_x, w_bc, w_dt, dt_bias, decay_rate, gain, cotangent, counts):
    seq_tokens = tokens[0]
    cot_rows = cotangent[0]
    row_total = seq_tokens.shape[0]
    slot_count = row_total // L
    state_size = w_bc.shape[1] // 2
    head_count = decay_rate.shape[0]
    head_size = w_x.shape[1] // head_count
    group_index = lax.axis_index("seq")
    filled = jnp.sum(jnp.where(jnp.arange(counts.shape[0]) == group_index, counts, 0))
    slot_used = (jnp.arange(slot_count) < filled).astype(jnp.float32)
    ext_width = w_bc.shape[1] + w_dt.shape[1]
    ext_pad = -ext_width % (4 * LANES)
    w_ext = jnp.concatenate([w_bc, w_dt, jnp.zeros((w_dt.shape[0], ext_pad), w_dt.dtype)], axis=1)
    inner, ext = project(seq_tokens, w_x, w_ext, seq_size)
    b_proj = ext[:, :state_size].astype(jnp.bfloat16)
    c_proj = ext[:, state_size : 2 * state_size].astype(jnp.bfloat16)
    dt_raw = ext[:, 2 * state_size : 2 * state_size + head_count]
    dt_blocks = (
        jax.nn.softplus(dt_raw + dt_bias).reshape(slot_count, L, head_count)
        * slot_used[:, None, None]
    )
    cumulative = jnp.cumsum(dt_blocks * -decay_rate, axis=1)
    inner_blocks = inner.reshape(slot_count, L, -1)
    b_blocks = b_proj.reshape(slot_count, L, -1)
    c_blocks = c_proj.reshape(slot_count, L, -1)
    cot_blocks = cot_rows.reshape(slot_count, L, -1)
    running = jnp.zeros((state_size, inner.shape[1]), jnp.float32)
    passed = jnp.ones((1, inner.shape[1]), jnp.float32)
    priors = []
    for slot in range(slot_count):
        priors.append((running, passed))
        decay = jnp.repeat(jnp.exp(cumulative[slot, -1]), head_size)[None, :]
        addition = stretch_state(
            inner_blocks[slot], b_blocks[slot], cumulative[slot], dt_blocks[slot], head_size
        )
        running = running * decay + addition
        passed = passed * decay
    enter = entering(
        running.astype(jnp.bfloat16), jnp.broadcast_to(passed, (8, passed.shape[1])), seq_size
    )
    outputs, grads = [], []
    for slot in range(slot_count):
        prior, through = priors[slot]
        state_low = (enter.astype(jnp.float32) * through + prior).astype(jnp.bfloat16)
        output, grad = stretch_outputs(
            inner_blocks[slot], b_blocks[slot], c_blocks[slot], cumulative[slot], dt_blocks[slot],
            state_low, gain, cot_blocks[slot], slot_used[slot],
        )
        outputs.append(output)
        grads.append(grad)
    ssm_output = jnp.concatenate(outputs, axis=0)
    grad_c_rows = jnp.concatenate(grads, axis=0)
    partial = jnp.dot(seq_tokens.T, grad_c_rows, preferred_element_type=jnp.float32)
    gradient = reduce_rows(partial.astype(jnp.bfloat16), seq_size, dp_size)
    return (ssm_output[None], gradient)


def solution(mesh):
    return jax.shard_map(
        functools.partial(body, mesh.shape["dp"], mesh.shape["seq"]),
        mesh=mesh,
        in_specs=(
            P("dp", "seq", None),
            P("seq", None),
            P("seq", None),
            P("seq", None),
            P(),
            P(),
            P(),
            P("dp", "seq", None),
            P(),
        ),
        out_specs=(P("dp", "seq", None), P("seq", None)),
        check_vma=False,
    )
```

time: 521 us -> 267 us (0.51)
  waiting for transfers between devices: 322 us -> 0 us
  Pallas kernels: 0 us -> 163 us
  blocking collectives: 29 us -> 0 us
  other arithmetic: 62.6 us -> 34.2 us
  local copies, waits for them, and re-layouts: 47.4 us -> 27.6 us
  between operations: 14.6 us -> 1.15 us
    all_gather x3 -> x0, waiting for transfers between devices: 247 us -> none  [the longest x1 139 us: body(): lax.all_gather(w_x, 'seq', axis=0, tiled=True)]
    pallas_call x0 -> x3, Pallas kernels: none -> 163 us  [the longest x1 95.8 us: project(): pl.pallas_call(functools.partial(project_kernel, seq_size, stages), out_s...]
    psum x1 -> x0, waiting for transfers between devices: 48 us -> none  [body(): gradient = lax.psum(partial_rows, 'dp').astype(jnp.float32)]
    unnamed x6 -> x0, waiting for transfers between devices: 27.4 us -> none
    select_n x7 -> x1, other arithmetic: 24.3 us -> 1.1 us  [body(): jax.nn.softplus(dt_raw + dt_bias).reshape(slot_count, L, head_count)]
    dynamic_slice x10 -> x0, local copies, waits for them, and re-layouts: 17.5 us -> none  [the longest x8 16.2 us: body(): lax.map(lambda stretch_data: stretch_state(stretch_data[0], stretch_data[...]
    all_gather x1 -> x0, blocking collectives: 16 us -> none  [body(): lax.all_gather(w_dt, 'seq', axis=0, tiled=True)]
    unnamed x1 -> x0, blocking collectives: 13 us -> none
  transfers between devices with their start and end apart: 5 -> 0, of which waited for: 5 -> 0; matrix products, arithmetic and copies ran while one was open for 1% -> 0% of each run, Pallas kernels for 0% -> 0%
where the time goes in v1:
time: 267 us
  Pallas kernels  163 us (61%)
  matrix products  41.2 us (15%)
  other arithmetic  34.2 us (13%)
  local copies, waits for them, and re-layouts  27.6 us (10%)
    pallas_call x1, Pallas kernels, project(): pl.pallas_call(functools.partial(project_kernel, seq_size, stages), out_s...  95.8 us
    pallas_call x1, Pallas kernels, entering(): pl.pallas_call(functools.partial(entering_kernel, seq_size), out_shape=ja...  41.6 us
    pallas_call x1, Pallas kernels, reduce_rows(): pl.pallas_call(functools.partial(reduce_kernel, seq_size, dp_size), out_s...  25.2 us
    dot_general x2, matrix products, stretch_outputs(): jnp.einsum('hts,shp->thp', mixing, inner_heads, preferred_element_type=jn...  14.2 us
    mul x2, other arithmetic, stretch_outputs(): full * jnp.sum(grad_out * full, axis=2, keepdims=True)  13.8 us
    dot_general x2, matrix products, stretch_outputs(): jnp.einsum('thp,shp->hts', grad_low, inner_heads, preferred_element_type=...  9.39 us
    dot_general x2, matrix products, stretch_state(): return jnp.dot(b_proj.T, scaled, preferred_element_type=jnp.float32)  6.8 us
    convert_element_type x2, local copies, waits for them, and re-layouts, stretch_outputs(): grad_out = cot_rows.reshape(length, head_count, head_size) * gain_heads  5.99 us

profile of v1, /device:TPU:9, one launch (start us, length us, event | category | flops | bytes accessed | tf_op | source)
XLA Modules:
  0.0 266.8 jit_solution(16679946039613477463)
XLA Ops:
  0.6 0.0 copy-start.23
  0.6 0.9 copy.45
  1.5 0.1 pad.6.clone
  1.6 1.7 maximum_maximum_fusion.we_ref
  3.3 95.8 %project.1 = (bf16[512,3072]{1,0:T(8,128)(2,1)}, f32[512,512]{1,0:T(8,128)}) custom-call(bf16[512,2560]{1,0:T(8,128)(2,1)} %bitcast.85, bf16[320,3072]{1,0:T(8,128)(2,1)} %wm_ref.1, bf16[320,512]{1,0:T(8,128)(2,1)} %maximum_maximum_fusion.we_ref), custom_call_target="tpu_custom_call" | custom-call | tf_op jit(solution)/shard_map/project/pallas_call | solution.py:156
  99.2 1.1 compare_select_fusion
  100.3 0.1 copy.47
  100.4 0.0 copy-done.24
  100.4 0.6 fusion.57
  101.1 0.6 compare_convert_fusion
  101.7 0.1 multiply_bitcast_fusion
  101.8 1.2 reduce-window.6
  103.0 0.2 slice_reduce_fusion
  103.3 0.1 bitcast_bitcast_fusion
  103.4 0.2 slice_reduce_fusion.1
  103.5 0.6 bitcast_exponential_fusion.1
  104.2 0.2 broadcast_in_dim.77
  104.4 2.4 copy.50
  106.8 0.1 broadcast_in_dim.42
  106.9 0.1 mul.227
  107.0 0.1 broadcast_in_dim.78
  107.0 0.1 mul.231
  107.1 1.3 convert.6
  108.4 3.0 %convolution_add_fusion.1 = f32[128,3072]{1,0:T(8,128)S(1)} fusion(f32[256,3072]{1,0:T(8,128)} %copy.50, f32[3072]{0:T(1024)S(1)} %get-tuple-element.31, bf16[512,512]{1,0:T(8,128)(2,1)S(1)} %convert.6, bf16[512,3072]{1,0:T(8,128)(2,1)} %get-tuple-element.4), kind=kOutput, calls=%fused_computation.23 | convolution fusion | flops 204079104 | bytes 6369280 | tf_op jit(solution)/shard_map/dot_general | solution.py:353
  111.5 1.9 broadcast_in_dim.79
  113.4 3.6 %copy.51 = f32[256,3072]{1,0:T(8,128)} copy(f32[256,3072]{0,1:T(8,128)} %bitcast.84) | data formatting | bytes 6291456 | tf_op jit(solution)/shard_map/reshape | solution.py:352
  117.0 3.8 %fusion.16.add_ref = bf16[128,3072]{1,0:T(8,128)(2,1)} fusion(f32[256,3072]{1,0:T(8,128)} %copy.51, f32[128,3072]{1,0:T(8,128)S(1)} %convolution_add_fusion.1, f32[3072]{0:T(1024)S(1)} %mul.231, bf16[512,512]{1,0:T(8,128)(2,1)S(1)} %convert.6, bf16[512,3072]{1,0:T(8,128)(2,1)} %get-tuple-element.4), kind=kOutput, calls=%fused_computation.24 | convolution fusion | flops 204865536 | bytes 7155712 | tf_op jit(solution)/shard_map/dot_general | solution.py:353
  120.7 0.6 broadcast_in_dim.80.decay_ref
  121.4 41.6 %entering.1 = bf16[128,3072]{1,0:T(8,128)(2,1)} custom-call(bf16[128,3072]{1,0:T(8,128)(2,1)} %fusion.16.add_ref, f32[8,3072]{1,0:T(8,128)} %broadcast_in_dim.80.decay_ref), custom_call_target="tpu_custom_call" | custom-call | tf_op jit(solution)/shard_map/entering/pallas_call | solution.py:246
  162.9 3.6 %fusion.43 = f32[256,3072]{0,1:T(8,128)} fusion(bf16[128,3072]{1,0:T(8,128)(2,1)} %entering.1, bf16[512,512]{1,0:T(8,128)(2,1)S(1)} %convert.6), kind=kOutput, calls=%fused_computation.78 | convolution fusion | flops 201326592 | bytes 3997696 | tf_op jit(solution)/shard_map/dot_general | solution.py:367
  166.5 0.7 slice_bitcast_fusion.1
  167.2 0.2 fusion.45
  167.4 1.4 fusion.64
  168.7 2.6 copy.46
  171.4 0.0 copy-start.13
  171.4 0.0 copy-start.22
  171.4 7.0 %multiply_reduce_fusion.5 = (f32[256,48]{0,1:T(8,128)S(1)}, f32[256,48,64]{0,2,1:T(8,128)}) fusion(f32[256,48,64]{0,2,1:T(8,128)} %bitcast.90, f32[256,48]{0,1:T(8,128)S(1)} %get-tuple-element.16, bf16[256,48,64]{0,2,1:T(8,128)(2,1)} %bitcast.92, f32[48,256]{1,0:T(8,128)} %get-tuple-element.22, f32[48,256]{1,0:T(8,128)} %get-tuple-element.43, ...), kind=kOutput, calls=%fused_computation.41 | convolution fusion | flops 421515264 | bytes 8388608 | tf_op jit(solution)/shard_map/hts,shp->thp/dot_general | solution.py:364
  178.5 0.6 fusion.66
  179.1 0.1 mul.240
  179.1 5.4 %slice_convert_fusion.1 = (f32[1,256,3072]{2,1,0:T(8,128)}, f32[1,256,3072]{2,1,0:T(8,128)}) fusion(bf16[1,512,3072]{2,1,0:T(8,128)(2,1)} %param.16), kind=kLoop, calls=%fused_computation.49 | loop fusion | flops 1572864 | bytes 9437184 | tf_op jit(solution)/shard_map/convert_element_type | solution.py:376
  184.5 3.6 %copy.57 = f32[1,256,3072]{1,2,0:T(8,128)} copy(f32[1,256,3072]{2,1,0:T(8,128)} %get-tuple-element.10) | data formatting | bytes 6291456 | tf_op jit(solution)/shard_map/convert_element_type | solution.py:376
  188.1 6.8 %multiply_convert_fusion.5 = (bf16[256,48,64]{0,2,1:T(8,128)(2,1)S(1)}, bf16[256,48,64]{0,2,1:T(8,128)(2,1)S(1)}) fusion(f32[256,48]{0,1:T(8,128)S(1)} %copy-done.19, f32[]{:T(128)} %bitcast.16, f32[256,48]{0,1:T(8,128)S(1)} %get-tuple-element.24, f32[256,48,64]{0,2,1:T(8,128)} %get-tuple-element.35, f32[256,48,64]{0,2,1:T(8,128)} %bitcast.88, ...), kind=kOutput, calls=%fused_computation.34 | output fusion | flops 8663103 | bytes 9596932 | tf_op jit(solution)/shard_map/mul | solution.py:379
  195.0 4.8 %multiply_reduce_fusion.1 = bf16[256,256]{1,0:T(8,128)(2,1)S(1)} fusion(f32[48,256]{1,0:T(8,128)S(1)} %copy-done.20, f32[48,256]{1,0:T(8,128)S(1)} %copy-done.21, pred[256,256]{1,0:T(8,128)(4,1)S(1)} %iota_compare_fusion, bf16[256,48,64]{0,2,1:T(8,128)(2,1)S(1)} %bitcast.93, bf16[256,48,64]{0,2,1:T(8,128)(2,1)S(1)} %get-tuple-element.41), kind=kOutput, calls=%fused_computation.3 | convolution fusion | flops 418316288 | bytes 3440640 | tf_op jit(solution)/shard_map/thp,shp->hts/dot_general | solution.py:382
  199.8 0.2 fusion.37
  200.0 0.6 fusion.30
  200.6 0.2 add_convert_fusion
  200.8 0.9 copy-done.4
  201.7 2.3 fusion.39
  204.0 0.2 fusion.41
  204.2 1.6 copy.53
  205.8 7.2 %multiply_reduce_fusion.4 = (f32[256,48]{0,1:T(8,128)S(1)}, f32[256,48,64]{0,2,1:T(8,128)}) fusion(f32[256,48,64]{0,2,1:T(8,128)} %bitcast.91, f32[256,48]{0,1:T(8,128)} %get-tuple-element.17, bf16[256,48,64]{0,2,1:T(8,128)(2,1)} %bitcast.94, f32[48,256]{1,0:T(8,128)} %get-tuple-element.23, f32[48,256]{1,0:T(8,128)} %get-tuple-element.42, ...), kind=kOutput, calls=%fused_computation.39 | convolution fusion | flops 421515264 | bytes 8388608 | tf_op jit(solution)/shard_map/hts,shp->thp/dot_general | solution.py:364
  213.0 2.4 copy.58
  215.4 7.0 %multiply_convert_fusion.4 = (bf16[256,48,64]{0,2,1:T(8,128)(2,1)S(1)}, bf16[256,48,64]{0,2,1:T(8,128)(2,1)S(1)}) fusion(f32[256,48]{0,1:T(8,128)S(1)} %copy-done.15, f32[]{:T(128)} %bitcast.24, f32[256,48]{0,1:T(8,128)S(1)} %get-tuple-element.26, f32[256,48,64]{0,2,1:T(8,128)} %get-tuple-element.37, f32[256,48,64]{0,2,1:T(8,128)} %bitcast.89, ...), kind=kOutput, calls=%fused_computation.30 | output fusion | flops 8663103 | bytes 9596932 | tf_op jit(solution)/shard_map/mul | solution.py:379
  222.5 4.6 %multiply_reduce_fusion = bf16[256,256]{1,0:T(8,128)(2,1)S(1)} fusion(f32[48,256]{1,0:T(8,128)S(1)} %copy-done.16, f32[48,256]{1,0:T(8,128)S(1)} %copy-done.17, pred[256,256]{1,0:T(8,128)(4,1)S(1)} %copy-done.14, bf16[256,48,64]{0,2,1:T(8,128)(2,1)S(1)} %bitcast.95, bf16[256,48,64]{0,2,1:T(8,128)(2,1)S(1)} %get-tuple-element.39), kind=kOutput, calls=%fused_computation.2 | convolution fusion | flops 418316288 | bytes 3440640 | tf_op jit(solution)/shard_map/thp,shp->hts/dot_general | solution.py:382
  227.1 0.0 copy-start.3
  227.1 1.2 fusion.35
  228.3 0.6 fusion.31
  228.9 2.0 fusion.17.part_ref
  231.0 25.2 %reduce_rows.1 = f32[320,128]{1,0:T(8,128)} custom-call(bf16[2560,128]{1,0:T(8,128)(2,1)} %fusion.17.part_ref), custom_call_target="tpu_custom_call" | custom-call | tf_op jit(solution)/shard_map/reduce_rows/pallas_call | solution.py:320
  256.2 5.4 %multiply_convert_fusion.7 = (bf16[256,48,64]{0,2,1:T(8,128)(2,1)S(1)}, bf16[256,48,64]{0,2,1:T(8,128)(2,1)}) fusion(f32[256,48,64]{0,2,1:T(8,128)} %get-tuple-element.35, f32[]{:T(128)} %bitcast.16, f32[48,64]{1,0:T(8,128)S(1)} %copy-done.12, f32[256,48]{0,1:T(8,128)S(1)} %get-tuple-element.25, f32[]{:T(128)} %bitcast.24, ...), kind=kLoop, calls=%fused_computation.40 | loop fusion | flops 6291456 | bytes 9547784 | tf_op jit(solution)/shard_map/convert_element_type | solution.py:375
  261.7 0.9 copy.55
  262.5 1.7 copy.56
  264.3 1.9 maximum_bitcast_fusion
  266.1 0.7 copy.69
  (57 shorter events, 0.2 us)
Async XLA Ops:
  0.6 98.6 %copy-start.23 = (f32[48]{0:T(128)S(1)}, f32[48]{0:T(128)}, u32[]{:S(2)}) copy-start(f32[48]{0:T(128)} %param.13) | copy-start | bytes 580
  1.6 98.8 %copy-start.24 = (s32[8]{0:T(128)S(1)}, s32[8]{0:T(128)}, u32[]{:S(2)}) copy-start(s32[8]{0:T(128)} %param.17) | copy-start | bytes 100
  1.6 100.1 %copy-start.25 = (f32[48]{0:T(128)S(1)}, f32[48]{0:T(128)}, u32[]{:S(2)}) copy-start(f32[48]{0:T(128)} %param.14) | copy-start | bytes 580
  104.2 67.2 %copy-start.18 = (f32[256,48]{0,1:T(8,128)}, f32[256,48]{0,1:T(8,128)S(1)}, u32[]{:S(2)}) copy-start(f32[256,48]{0,1:T(8,128)S(1)} %get-tuple-element.16) | copy-start | bytes 147460
  108.4 58.8 %copy-start.6 = (bf16[512,512]{1,0:T(8,128)(2,1)}, bf16[512,512]{1,0:T(8,128)(2,1)S(1)}, u32[]{:S(2)}) copy-start(bf16[512,512]{1,0:T(8,128)(2,1)S(1)} %convert.6) | copy-start | bytes 1572868
  162.9 4.5 %copy-start.1 = (bf16[512,3072]{1,0:T(8,128)(2,1)S(1)}, bf16[512,3072]{1,0:T(8,128)(2,1)}, u32[]{:S(2)}) copy-start(bf16[512,3072]{1,0:T(8,128)(2,1)} %get-tuple-element.4) | copy-start | bytes 9437188
  171.4 23.5 %copy-start.13 = (pred[256,256]{1,0:T(8,128)(4,1)}, pred[256,256]{1,0:T(8,128)(4,1)S(1)}, u32[]{:S(2)}) copy-start(pred[256,256]{1,0:T(8,128)(4,1)S(1)} %iota_compare_fusion) | copy-start | bytes 196612
  171.4 7.6 %copy-start.22 = (f32[3072]{0:T(1024)S(1)}, f32[3072]{0:T(1024)}, u32[]{:S(2)}) copy-start(f32[3072]{0:T(1024)} %param.15) | copy-start | bytes 36868
  179.1 9.0 %copy-start.11 = (f32[48,64]{1,0:T(8,128)}, f32[48,64]{1,0:T(8,128)S(1)}, u32[]{:S(2)}) copy-start(f32[48,64]{1,0:T(8,128)S(1)} %mul.240) | copy-start | bytes 36868
  184.5 3.6 %copy-start.19 = (f32[256,48]{0,1:T(8,128)S(1)}, f32[256,48]{0,1:T(8,128)}, u32[]{:S(2)}) copy-start(f32[256,48]{0,1:T(8,128)} %copy-done.18) | copy-start | bytes 147460
  188.1 6.9 %copy-start.8 = (bf16[256,3072]{0,1:T(8,128)(2,1)S(1)}, bf16[256,3072]{0,1:T(8,128)(2,1)}, u32[]{:S(2)}) copy-start(bf16[256,3072]{0,1:T(8,128)(2,1)} %copy.46) | copy-start | bytes 4718596
  188.1 6.9 %copy-start.20 = (f32[48,256]{1,0:T(8,128)S(1)}, f32[48,256]{1,0:T(8,128)}, u32[]{:S(2)}) copy-start(f32[48,256]{1,0:T(8,128)} %get-tuple-element.22) | copy-start | bytes 147460
  188.1 6.9 %copy-start.21 = (f32[48,256]{1,0:T(8,128)S(1)}, f32[48,256]{1,0:T(8,128)}, u32[]{:S(2)}) copy-start(f32[48,256]{1,0:T(8,128)} %get-tuple-element.43) | copy-start | bytes 147460
  195.0 4.8 %copy-start.7 = (bf16[512,512]{1,0:T(8,128)(2,1)S(1)}, bf16[512,512]{1,0:T(8,128)(2,1)}, u32[]{:S(2)}) copy-start(bf16[512,512]{1,0:T(8,128)(2,1)} %copy-done.6) | copy-start | bytes 1572868
  195.0 5.0 %copy-start.2 = (bf16[128,3072]{1,0:T(8,128)(2,1)S(1)}, bf16[128,3072]{1,0:T(8,128)(2,1)}, u32[]{:S(2)}) copy-start(bf16[128,3072]{1,0:T(8,128)(2,1)} %entering.1) | copy-start | bytes 2359300
  200.8 0.9 copy-start.4
  205.8 7.2 %copy-start = (f32[1,256,3072]{2,1,0:T(8,128)S(1)}, f32[1,256,3072]{2,1,0:T(8,128)}, u32[]{:S(2)}) copy-start(f32[1,256,3072]{2,1,0:T(8,128)} %get-tuple-element.11) | copy-start | bytes 9437188
  213.0 2.4 copy-start.12
  213.0 2.4 copy-start.15
  215.4 7.0 %copy-start.9 = (bf16[256,3072]{0,1:T(8,128)(2,1)S(1)}, bf16[256,3072]{0,1:T(8,128)(2,1)}, u32[]{:S(2)}) copy-start(bf16[256,3072]{0,1:T(8,128)(2,1)} %copy.53) | copy-start | bytes 4718596
  215.4 7.0 %copy-start.14 = (pred[256,256]{1,0:T(8,128)(4,1)S(1)}, pred[256,256]{1,0:T(8,128)(4,1)}, u32[]{:S(2)}) copy-start(pred[256,256]{1,0:T(8,128)(4,1)} %copy-done.13) | copy-start | bytes 196612
  215.4 7.0 %copy-start.16 = (f32[48,256]{1,0:T(8,128)S(1)}, f32[48,256]{1,0:T(8,128)}, u32[]{:S(2)}) copy-start(f32[48,256]{1,0:T(8,128)} %get-tuple-element.23) | copy-start | bytes 147460
  215.4 7.0 %copy-start.17 = (f32[48,256]{1,0:T(8,128)S(1)}, f32[48,256]{1,0:T(8,128)}, u32[]{:S(2)}) copy-start(f32[48,256]{1,0:T(8,128)} %get-tuple-element.42) | copy-start | bytes 147460
  222.5 5.8 %copy-start.5 = (bf16[128,3072]{1,0:T(8,128)(2,1)S(1)}, bf16[128,3072]{1,0:T(8,128)(2,1)}, u32[]{:S(2)}) copy-start(bf16[128,3072]{1,0:T(8,128)(2,1)} %copy-done.4) | copy-start | bytes 2359300
  227.1 1.8 copy-start.3
  264.2 1.9 copy-start.10

commit v2 on v1

--- a/solution.py
+++ b/solution.py
@@ -339,54 +339,127 @@
     )(partial)
 
 
-def decay_weights(cumulative, dt_rows):
-    length = cumulative.shape[0]
-    causal = jnp.arange(length)[:, None] >= jnp.arange(length)[None, :]
-    gap_log = cumulative.T[:, :, None] - cumulative.T[:, None, :]
-    gap_log = jnp.where(causal[None, :, :], gap_log, -jnp.inf)
-    return jnp.exp(gap_log) * dt_rows.T[:, None, :]
-
-
 def stretch_state(inner, b_proj, cumulative, dt_rows, head_size):
     to_end = jnp.exp(cumulative[-1][None, :] - cumulative) * dt_rows
     scaled = (inner * jnp.repeat(to_end, head_size, axis=1)).astype(jnp.bfloat16)
     return jnp.dot(b_proj.T, scaled, preferred_element_type=jnp.float32)
 
 
-def stretch_outputs(inner, b_proj, c_proj, cumulative, dt_rows, state_low, gain, cot_rows, used):
-    length = inner.shape[0]
-    head_count = cumulative.shape[1]
-    head_size = inner.shape[1] // head_count
-    weights = decay_weights(cumulative, dt_rows)
-    gram_mat = jnp.dot(c_proj, b_proj.T, preferred_element_type=jnp.float32)
-    mixing = (gram_mat[None, :, :] * weights).astype(jnp.bfloat16)
-    inner_heads = inner.reshape(length, head_count, head_size)
-    y_intra = jnp.einsum("hts,shp->thp", mixing, inner_heads, preferred_element_type=jnp.float32)
-    growth = jnp.exp(cumulative)[:, :, None]
-    y_inter = (
-        jnp.dot(c_proj, state_low, preferred_element_type=jnp.float32).reshape(
-            length, head_count, head_size
+def outputs_kernel(
+    head_size, used_ref, b_ref, c_ref, inner_ref, cot_ref, cum_ref, cum_row_ref, dt_row_ref,
+    state_ref, gain_ref, out_ref, grad_ref, gram, combined, carried,
+):
+    slot, pair = pl.program_id(0), pl.program_id(1)
+
+    @pl.when(pair == 0)
+    def _():
+        gram[...] = lax.dot_general(
+            c_ref[...], b_ref[...], (((1,), (1,)), ((), ())), preferred_element_type=jnp.float32
         )
-        * growth
-    )
-    full = y_intra + y_inter
-    radius = jnp.sqrt(jnp.mean(full * full, axis=2, keepdims=True) + norm_floor)
-    gain_heads = gain.reshape(head_count, head_size)
-    output = (full / radius * gain_heads * used).reshape(length, -1).astype(jnp.bfloat16)
-    grad_out = cot_rows.reshape(length, head_count, head_size) * gain_heads
-    grad_full = (
-        grad_out / radius
-        - full * jnp.sum(grad_out * full, axis=2, keepdims=True) / (head_size * radius**3)
-    ) * used
-    grad_low = grad_full.astype(jnp.bfloat16)
-    intersect = jnp.einsum(
-        "thp,shp->hts", grad_low, inner_heads, preferred_element_type=jnp.float32
-    )
-    combined = jnp.sum(intersect * weights, axis=0).astype(jnp.bfloat16)
-    grad_intra = jnp.dot(combined, b_proj, preferred_element_type=jnp.float32)
-    scaled_grad = (grad_full * growth).reshape(length, -1).astype(jnp.bfloat16)
-    grad_inter = jnp.dot(scaled_grad, state_low.T, preferred_element_type=jnp.float32)
-    return (output, (grad_intra + grad_inter).astype(jnp.bfloat16))
+        combined[...] = jnp.zeros_like(combined)
+        carried[...] = jnp.zeros_like(carried)
+
+    length, width = inner_ref.shape
+    heads = width // head_size
+    used = used_ref[slot]
+    inner = inner_ref[...]
+    state = state_ref[0]
+    lane_head = lax.broadcasted_iota(jnp.int32, (length, width), 1) // head_size
+    causal = lax.broadcasted_iota(jnp.int32, (length, length), 0) >= lax.broadcasted_iota(
+        jnp.int32, (length, length), 1
+    )
+
+    def spread(columns):
+        result = columns[0]
+        for head in range(1, heads):
+            result = jnp.where(lane_head == head, columns[head], result)
+        return jnp.broadcast_to(result, (length, width))
+
+    def head_sums(values):
+        return spread([
+            jnp.sum(jnp.where(lane_head == head, values, 0.0), axis=1, keepdims=True)
+            for head in range(heads)
+        ])
+
+    weights = []
+    intra = []
+    for head in range(heads):
+        gap = cum_ref[0, 0, :, head : head + 1] - cum_row_ref[0, 0, head : head + 1, :]
+        weight = jnp.exp(jnp.where(causal, gap, -jnp.inf)) * dt_row_ref[0, 0, head : head + 1, :]
+        weights.append(weight)
+        mixing = (gram[...] * weight).astype(jnp.bfloat16)
+        intra.append(jnp.dot(mixing, inner, preferred_element_type=jnp.float32))
+    growth = spread([jnp.exp(cum_ref[0, 0, :, head : head + 1]) for head in range(heads)])
+    full = spread(intra) + growth * jnp.dot(c_ref[...], state, preferred_element_type=jnp.float32)
+    inverse = 1.0 / jnp.sqrt(head_sums(full * full) * (1.0 / head_size) + norm_floor)
+    gain = gain_ref[...]
+    out_ref[...] = (full * inverse * gain * used).astype(jnp.bfloat16)
+    grad_out = cot_ref[...].astype(jnp.float32) * gain
+    pull = head_sums(grad_out * full) * (1.0 / head_size)
+    grad_full = (grad_out * inverse - full * pull * (inverse * inverse * inverse)) * used
+    total = combined[...]
+    for head in range(heads):
+        grad_low = jnp.where(lane_head == head, grad_full, 0.0).astype(jnp.bfloat16)
+        intersect = lax.dot_general(
+            grad_low, inner, (((1,), (1,)), ((), ())), preferred_element_type=jnp.float32
+        )
+        total = total + intersect * weights[head]
+    combined[...] = total
+    carried[...] += lax.dot_general(
+        (grad_full * growth).astype(jnp.bfloat16), state, (((1,), (1,)), ((), ())),
+        preferred_element_type=jnp.float32,
+    )
+
+    @pl.when(pair == pl.num_programs(1) - 1)
+    def _():
+        grad_ref[...] = (
+            carried[...]
+            + jnp.dot(
+                combined[...].astype(jnp.bfloat16), b_ref[...], preferred_element_type=jnp.float32
+            )
+        ).astype(jnp.bfloat16)
+
+
+def stretch_outputs(inner, b_proj, c_proj, cumulative, dt_blocks, states, gain, cot_rows, used):
+    slots, length, head_count = cumulative.shape
+    width = inner.shape[1]
+    head_size = width // head_count
+    heads = LANES // head_size
+    pairs = head_count // heads
+    state_size = b_proj.shape[1]
+    cum_rows = cumulative.transpose(0, 2, 1).reshape(slots, pairs, heads, length)
+    dt_rows = dt_blocks.transpose(0, 2, 1).reshape(slots, pairs, heads, length)
+    cum_columns = cumulative.reshape(slots, length, pairs, heads).transpose(0, 2, 1, 3)
+    by_slot = pl.BlockSpec((length, state_size), lambda slot, pair: (slot, 0))
+    by_pair = pl.BlockSpec((length, LANES), lambda slot, pair: (slot, pair))
+    row_spec = pl.BlockSpec((1, 1, heads, length), lambda slot, pair: (slot, pair, 0, 0))
+    return pl.pallas_call(
+        functools.partial(outputs_kernel, head_size),
+        grid=(slots, pairs),
+        out_shape=(
+            jax.ShapeDtypeStruct((slots * length, width), jnp.bfloat16),
+            jax.ShapeDtypeStruct((slots * length, state_size), jnp.bfloat16),
+        ),
+        in_specs=[
+            pl.BlockSpec(memory_space=pltpu.SMEM),
+            by_slot,
+            by_slot,
+            by_pair,
+            by_pair,
+            pl.BlockSpec((1, 1, length, heads), lambda slot, pair: (slot, pair, 0, 0)),
+            row_spec,
+            row_spec,
+            pl.BlockSpec((1, state_size, LANES), lambda slot, pair: (slot, 0, pair)),
+            pl.BlockSpec((1, LANES), lambda slot, pair: (0, pair)),
+        ],
+        out_specs=(by_pair, by_slot),
+        scratch_shapes=[
+            pltpu.VMEM((length, length), jnp.float32),
+            pltpu.VMEM((length, length), jnp.float32),
+            pltpu.VMEM((length, state_size), jnp.float32),
+        ],
+        name="outputs",
+    )(used, b_proj, c_proj, inner, cot_rows, cum_columns, cum_rows, dt_rows, states, gain[None, :])
 
 
 def body(dp_size, seq_size, tokens, w_x, w_bc, w_dt, dt_bias, decay_rate, gain, cotangent, counts):
@@ -414,8 +487,6 @@
     cumulative = jnp.cumsum(dt_blocks * -decay_rate, axis=1)
     inner_blocks = inner.reshape(slot_count, L, -1)
     b_blocks = b_proj.reshape(slot_count, L, -1)
-    c_blocks = c_proj.reshape(slot_count, L, -1)
-    cot_blocks = cot_rows.reshape(slot_count, L, -1)
     running = jnp.zeros((state_size, inner.shape[1]), jnp.float32)
     passed = jnp.ones((1, inner.shape[1]), jnp.float32)
     priors = []
@@ -430,18 +501,13 @@
     enter = entering(
         running.astype(jnp.bfloat16), jnp.broadcast_to(passed, (8, passed.shape[1])), seq_size
     )
-    outputs, grads = [], []
-    for slot in range(slot_count):
-        prior, through = priors[slot]
-        state_low = (enter.astype(jnp.float32) * through + prior).astype(jnp.bfloat16)
-        output, grad = stretch_outputs(
-            inner_blocks[slot], b_blocks[slot], c_blocks[slot], cumulative[slot], dt_blocks[slot],
-            state_low, gain, cot_blocks[slot], slot_used[slot],
-        )
-        outputs.append(output)
-        grads.append(grad)
-    ssm_output = jnp.concatenate(outputs, axis=0)
-    grad_c_rows = jnp.concatenate(grads, axis=0)
+    states = jnp.stack([
+        (enter.astype(jnp.float32) * through + prior).astype(jnp.bfloat16)
+        for prior, through in priors
+    ])
+    ssm_output, grad_c_rows = stretch_outputs(
+        inner, b_proj, c_proj, cumulative, dt_blocks, states, gain, cot_rows, slot_used
+    )
     partial = jnp.dot(seq_tokens.T, grad_c_rows, preferred_element_type=jnp.float32)
     gradient = reduce_rows(partial.astype(jnp.bfloat16), seq_size, dp_size)
     return (ssm_output[None], gradient)

time: 267 us -> 247 us (0.925)
  Pallas kernels: 163 us -> 208 us
  matrix products: 41.2 us -> 8.18 us
  other arithmetic: 34.2 us -> 11 us
  local copies, waits for them, and re-layouts: 27.6 us -> 16.7 us
    pallas_call x0 -> x1, Pallas kernels: none -> 45.6 us  [stretch_outputs(): pl.pallas_call(functools.partial(outputs_kernel, head_size), grid=(slots,...]
    dot_general x12 -> x0, matrix products: 32.4 us -> none  [the longest x2 14.2 us: stretch_outputs(): jnp.einsum('hts,shp->thp', mixing, inner_heads, preferred_element_type=jn...]
    mul x4 -> x1, other arithmetic: 13.8 us -> 0.09 us  [stretch_state(): to_end = jnp.exp(cumulative[-1][None, :] - cumulative) * dt_rows]
    convert_element_type x3 -> x0, other arithmetic: 11 us -> none  [the longest x1 5.43 us: stretch_outputs(): (full / radius * gain_heads * used).reshape(length, -1).astype(jnp.bfloat16)]
    convert_element_type x4 -> x0, local copies, waits for them, and re-layouts: 8.56 us -> none  [the longest x2 5.99 us: stretch_outputs(): grad_out = cot_rows.reshape(length, head_count, head_size) * gain_heads]
    slice x5 -> x2, local copies, waits for them, and re-layouts: 6.33 us -> 0.9 us  [the longest x1 0.72 us: body(): c_proj = ext[:, state_size:2 * state_size].astype(jnp.bfloat16)]
    broadcast_in_dim x2 -> x4, local copies, waits for them, and re-layouts: 2.15 us -> 5.21 us  [stretch_state(): jnp.repeat(to_end, head_size, axis=1)]
    another operation x4 -> x7, other arithmetic: 2.63 us -> 5.42 us  [the longest x2 2.71 us: body(): jnp.stack([(enter.astype(jnp.float32) * through + prior).astype(jnp.bfloa...]
where the time goes in v2:
time: 247 us; the launch traced here: 245 us
  Pallas kernels  208 us (84%)
  local copies, waits for them, and re-layouts  16.7 us (7%)
  other arithmetic  11 us (4%)
  matrix products  8.18 us (3%)
    pallas_call x1, Pallas kernels, project(): pl.pallas_call(functools.partial(project_kernel, seq_size, stages), out_s...  95.9 us
    pallas_call x1, Pallas kernels, stretch_outputs(): pl.pallas_call(functools.partial(outputs_kernel, head_size), grid=(slots,...  45.6 us
    pallas_call x1, Pallas kernels, entering(): pl.pallas_call(functools.partial(entering_kernel, seq_size), out_shape=ja...  41.5 us
    pallas_call x1, Pallas kernels, reduce_rows(): pl.pallas_call(functools.partial(reduce_kernel, seq_size, dp_size), out_s...  25.2 us
    dot_general x2, matrix products, stretch_state(): return jnp.dot(b_proj.T, scaled, preferred_element_type=jnp.float32)  5.3 us
    broadcast_in_dim x4, local copies, waits for them, and re-layouts, stretch_state(): jnp.repeat(to_end, head_size, axis=1)  5.21 us

profile of v2, /device:TPU:9, one launch (start us, length us, event | category | flops | bytes accessed | tf_op | source)
XLA Modules:
  0.0 245.0 jit_solution(6180719598916265371)
XLA Ops:
  0.6 1.3 fusion.13
  1.9 0.6 compare_convert_fusion.used_ref
  2.6 0.0 copy-start.5
  2.6 0.7 neg.8
  3.3 0.1 pad.4.clone
  3.3 0.9 copy.26
  4.2 1.7 maximum_maximum_fusion.we_ref
  5.9 0.0 copy-start.6
  5.9 95.9 %project.1 = (bf16[512,3072]{1,0:T(8,128)(2,1)}, f32[512,512]{1,0:T(8,128)}) custom-call(bf16[512,2560]{1,0:T(8,128)(2,1)} %bitcast.58, bf16[320,3072]{1,0:T(8,128)(2,1)} %wm_ref.1, bf16[320,512]{1,0:T(8,128)(2,1)} %maximum_maximum_fusion.we_ref), custom_call_target="tpu_custom_call" | custom-call | tf_op jit(solution)/shard_map/project/pallas_call | solution.py:156
  101.8 0.0 copy-done.6
  101.8 1.1 compare_select_fusion
  102.9 1.3 convert.4
  104.2 0.0 copy-start.4
  104.2 0.1 copy.27
  104.3 0.0 copy-done.5
  104.4 0.1 multiply_bitcast_fusion
  104.5 1.2 reduce-window.6
  105.7 0.2 slice_reduce_fusion
  105.9 0.1 bitcast_bitcast_fusion
  106.0 0.1 broadcast_add_fusion
  106.1 0.1 copy.29
  106.1 0.7 reduce_window_sum.21.cum_row_ref
  106.9 0.2 slice_reduce_fusion.1
  107.1 0.1 broadcast_in_dim.42
  107.2 0.1 mul.69
  107.2 0.1 broadcast_in_dim.46
  107.3 0.1 mul.73
  107.4 0.7 broadcast_in_dim.49.decay_ref
  108.0 0.1 fusion.7
  108.1 0.1 copy.30
  108.2 0.7 reshape.74.dt_row_ref
  108.9 0.7 fusion.15
  109.6 0.0 copy-done.4
  109.6 0.2 broadcast_in_dim.47
  109.9 2.4 copy.34
  112.3 0.2 broadcast_in_dim.44
  112.5 2.4 copy.33
  114.9 0.0 copy-start
  114.9 0.0 copy-start.1
  114.9 3.0 %convolution_add_fusion.1 = f32[128,3072]{1,0:T(8,128)S(1)} fusion(f32[256,3072]{1,0:T(8,128)} %copy.33, bf16[512,3072]{1,0:T(8,128)(2,1)} %get-tuple-element.7.inner_ref, f32[3072]{0:T(1024)S(1)} %get-tuple-element.19, bf16[512,512]{1,0:T(8,128)(2,1)} %copy-done.4), kind=kOutput, calls=%fused_computation.1 | convolution fusion | flops 204079104 | bytes 6369280 | tf_op jit(solution)/shard_map/dot_general | solution.py:345
  117.9 0.3 copy-done
  118.2 1.0 copy-done.1
  119.1 2.3 fusion.add_ref
  121.4 41.5 %entering.1 = bf16[128,3072]{1,0:T(8,128)(2,1)} custom-call(bf16[128,3072]{1,0:T(8,128)(2,1)} %fusion.add_ref, f32[8,3072]{1,0:T(8,128)} %broadcast_in_dim.49.decay_ref), custom_call_target="tpu_custom_call" | custom-call | tf_op jit(solution)/shard_map/entering/pallas_call | solution.py:246
  163.0 0.0 copy-start.3
  163.0 1.4 fusion.4
  164.4 0.0 copy-done.3
  164.4 1.3 pad_maximum_fusion.state_ref
  165.7 3.9 %copy.31 = f32[2,256,24,2]{3,1,2,0:T(8,128)} copy(f32[2,256,24,2]{1,0,3,2:T(2,128)S(1)} %bitcast.64) | data formatting | bytes 196608 | tf_op jit(solution)/shard_map/reshape | solution.py:432
  169.6 0.0 copy-start.2
  169.7 45.6 %outputs.1 = (bf16[512,3072]{1,0:T(8,128)(2,1)}, bf16[512,128]{1,0:T(8,128)(2,1)}) custom-call(f32[2]{0:T(128)} %copy-done.5, bf16[512,128]{1,0:T(8,128)(2,1)} %get-tuple-element.15.b_ref, bf16[512,128]{1,0:T(8,128)(2,1)} %get-tuple-element.14.c_ref, bf16[512,3072]{1,0:T(8,128)(2,1)} %get-tuple-element.7.inner_ref, bf16[512,3072]{1,0:T(8,128)(2,1)} %bitcast.60, ...), custom_call_target="tpu_custom_call" | custom-call | tf_op jit(solution)/shard_map/outputs/pallas_call | solution.py:436
  215.3 0.0 copy-done.2
  215.3 2.9 %fusion.1.part_ref = bf16[2560,128]{1,0:T(8,128)(2,1)} fusion(bf16[512,128]{1,0:T(8,128)(2,1)} %get-tuple-element.9, bf16[1,512,2560]{2,1,0:T(8,128)(2,1)S(1)} %copy-done.2), kind=kOutput, calls=%fused_computation.4 | convolution fusion | flops 335872000 | bytes 3407872 | tf_op jit(solution)/shard_map/dot_general | solution.py:511
  218.2 25.2 %reduce_rows.1 = f32[320,128]{1,0:T(8,128)} custom-call(bf16[2560,128]{1,0:T(8,128)(2,1)} %fusion.1.part_ref), custom_call_target="tpu_custom_call" | custom-call | tf_op jit(solution)/shard_map/reduce_rows/pallas_call | solution.py:320
  243.4 1.6 copy.43
  (7 shorter events, 0.1 us)
Async XLA Ops:
  2.6 101.8 %copy-start.5 = (f32[2]{0:T(128)}, f32[2]{0:T(128)S(1)}, u32[]{:S(2)}) copy-start(f32[2]{0:T(128)S(1)} %compare_convert_fusion.used_ref) | copy-start | bytes 28
  5.9 95.9 %copy-start.6 = (f32[48]{0:T(128)S(1)}, f32[48]{0:T(128)}, u32[]{:S(2)}) copy-start(f32[48]{0:T(128)} %param.13) | copy-start | bytes 580
  104.2 5.4 %copy-start.4 = (bf16[512,512]{1,0:T(8,128)(2,1)}, bf16[512,512]{1,0:T(8,128)(2,1)S(1)}, u32[]{:S(2)}) copy-start(bf16[512,512]{1,0:T(8,128)(2,1)S(1)} %convert.4) | copy-start | bytes 1572868
  114.9 3.3 %copy-start = (f32[256,3072]{1,0:T(8,128)S(1)}, f32[256,3072]{1,0:T(8,128)}, u32[]{:S(2)}) copy-start(f32[256,3072]{1,0:T(8,128)} %copy.34) | copy-start | bytes 9437188
  114.9 4.3 %copy-start.1 = (bf16[512,3072]{1,0:T(8,128)(2,1)S(1)}, bf16[512,3072]{1,0:T(8,128)(2,1)}, u32[]{:S(2)}) copy-start(bf16[512,3072]{1,0:T(8,128)(2,1)} %get-tuple-element.7.inner_ref) | copy-start | bytes 9437188
  163.0 1.4 copy-start.3
  169.6 45.6 %copy-start.2 = (bf16[1,512,2560]{2,1,0:T(8,128)(2,1)S(1)}, bf16[1,512,2560]{2,1,0:T(8,128)(2,1)}, u32[]{:S(2)}) copy-start(bf16[1,512,2560]{2,1,0:T(8,128)(2,1)} %param.9) | copy-start | bytes 7864324
